TPU v7x, 512 devices: a whole 4x4x16 slice. The times are simulated.
512 devices in a mesh: tile: 16 (over y, x), depth: 32 (over z, core).
Axes of the slice: x: 4, y: 4, z: 16, core: 2. Of those that a mesh axis runs over, the one named last changes fastest.
Arguments:
- patches: float32 [1024, 256, 256], P('tile', 'depth'), may hold values from -6 to 6
- patch_owner: int32 [1024, 1], P('tile'), may hold values from 0 to 15; in each aligned block of 64 rows (0 to 63, 64 to 127, ...) at most 8 rows name the same one
- patch_level: int32 [1024], P('tile'), may hold values from 0 to 63
- phases: float32 [1024, 256, 256], P('tile', None, 'depth'), may hold values from -3.140625 to 3.140625
Outputs:
- intensity: float32 [1024, 256, 256], P('tile', 'depth')
Inputs may be any that keep to these rules, and one draw needn't show every extreme that they name: `patch_owner`: among the 64 patches of one index of tile, at most 8 have the same owner.
All inputs are finite; a program needn't handle non-finite values.
Results may differ from a plain program's by a relative error of at most 0.00017.
Values sent between devices are 32-bit elements; how exact they have to be, the bound alone decides.
A program may use at most 64 MiB of HBM per device.

v0:
```python
import math
import jax
import jax.numpy as jnp
from jax import lax
from jax.sharding import PartitionSpec as P

HIGHEST_PRECISION = lax.Precision.HIGHEST


def sent_together(arrays, axis, split_dim, concat_dim, along):
    widths = [a.shape[along] for a in arrays]
    both = jnp.concatenate(arrays, axis=along)
    filled = lax.all_to_all(both, axis, split_axis=split_dim, concat_axis=concat_dim, tiled=True)
    return tuple(jnp.split(filled, [sum(widths[:k]) for k in range(1, len(widths))], axis=along))


def tables(extent):
    indices = jnp.arange(extent, dtype=jnp.int32)
    product = indices[:, None] * indices[None, :] % extent
    angles = product.astype(jnp.float32) * (2.0 * math.pi / extent)
    return (jnp.cos(angles), jnp.sin(angles))


def right_apply(values, matrix):
    return jnp.einsum(
        "src,ck->srk",
        values,
        matrix,
        precision=HIGHEST_PRECISION,
        preferred_element_type=jnp.float32,
    )


def apply_rows(matrix, values):
    return jnp.einsum(
        "jk,skc->sjc",
        matrix,
        values,
        precision=HIGHEST_PRECISION,
        preferred_element_type=jnp.float32,
    )


def refocus(field, real_gain, imag_gain):
    extent = field.shape[2]
    cosine_table, sine_table = tables(extent)
    col_real = right_apply(field, cosine_table)
    col_imag = -right_apply(field, sine_table)
    col_real, col_imag = sent_together((col_real, col_imag), "depth", 2, 1, 0)
    spec_real = apply_rows(cosine_table, col_real) + apply_rows(sine_table, col_imag)
    spec_imag = apply_rows(cosine_table, col_imag) - apply_rows(sine_table, col_real)
    prop_real = spec_real * real_gain - spec_imag * imag_gain
    prop_imag = spec_real * imag_gain + spec_imag * real_gain
    back_real = apply_rows(cosine_table, prop_real) - apply_rows(sine_table, prop_imag)
    back_imag = apply_rows(cosine_table, prop_imag) + apply_rows(sine_table, prop_real)
    back_real, back_imag = sent_together((back_real, back_imag), "depth", 1, 2, 0)
    field_real = right_apply(back_real, cosine_table) - right_apply(back_imag, sine_table)
    field_imag = right_apply(back_real, sine_table) + right_apply(back_imag, cosine_table)
    return (field_real * field_real + field_imag * field_imag) * (1.0 / float(extent) ** 4)


def select_gains(selector, phase_block, lead):
    flattened = phase_block.reshape(phase_block.shape[0], -1)
    real_gain = jnp.dot(
        selector,
        jnp.cos(flattened),
        precision=HIGHEST_PRECISION,
        preferred_element_type=jnp.float32,
    )
    imag_gain = jnp.dot(
        selector,
        jnp.sin(flattened),
        precision=HIGHEST_PRECISION,
        preferred_element_type=jnp.float32,
    )
    shape_out = (lead, phase_block.shape[1], phase_block.shape[2])
    return (real_gain.reshape(shape_out), imag_gain.reshape(shape_out))


def on_device(patches, patch_owner, patch_level, phases):
    patch_count, row_count, extent = patches.shape
    levels = phases.shape[0]
    owners = lax.axis_size("tile")
    owner_column = patch_owner[:, 0]
    gathered = lax.all_gather(phases, "tile", axis=0, tiled=True)
    depth_index = owner_column * levels + patch_level
    depth_hot = (
        depth_index[:, None] == jnp.arange(owners * levels, dtype=jnp.int32)[None, :]
    ).astype(jnp.float32)
    real_gain, imag_gain = select_gains(depth_hot, gathered, patch_count)
    return refocus(patches, real_gain, imag_gain)


def solution(mesh):
    return jax.shard_map(
        on_device,
        mesh=mesh,
        in_specs=(P("tile", "depth", None), P("tile", None), P("tile"), P("tile", None, "depth")),
        out_specs=P("tile", "depth", None),
        check_vma=False,
    )
```

profile of v0, /device:TPU:1, one launch (start us, length us, event | category | flops | bytes accessed | tf_op | source)
XLA Modules:
  0.0 253.1 jit_solution(1416911551636459273)
XLA Ops:
  6.5 0.7 all-gather.2.cloned.1.call-update
  7.6 1.6 fusion.4
  9.2 1.6 convolution_bitcast_fusion
  10.9 1.4 copy.66
  12.3 17.0 %all-to-all-start = ((f32[128,8,256]{0,1,2:T(8,128)}), f32[128,8,256]{0,1,2:T(8,128)S(1)}, u32[]{:S(2)}, u32[]{:S(2)}) async-start(f32[128,8,256]{0,1,2:T(8,128)} %copy.66), calls=%async_computation | async-start | bytes 2097152 | tf_op jit(solution)/shard_map/all_to_all | solution.py:13
  29.4 55.5 %all-to-all-done = f32[128,8,256]{0,1,2:T(8,128)S(1)} async-done(((f32[128,8,256]{0,1,2:T(8,128)}), f32[128,8,256]{0,1,2:T(8,128)S(1)}, u32[]{:S(2)}, u32[]{:S(2)}) %all-to-all-start) | async-done | bytes 1048608 | tf_op jit(solution)/shard_map/all_to_all | solution.py:13
  86.7 1.6 fusion.35
  88.2 2.4 fusion.33
  90.6 1.6 fusion.12
  92.1 9.5 %all-gather.2.cloned.1.call-done = f32[1024,256,8]{1,2,0:T(8,128)} async-done(((f32[64,256,8]{1,2,0:T(8,128)}), f32[1024,256,8]{1,2,0:T(8,128)}) %all-gather.2.cloned.1.call-update) | async-done | bytes 8388624 | tf_op jit(solution)/shard_map/all_gather | solution.py:85
  101.7 8.8 %copy.72 = f32[1024,256,8]{0,2,1:T(8,128)} copy(f32[1024,256,8]{1,2,0:T(8,128)} %all-gather.2.cloned.1.call-done) | data formatting | bytes 16777216 | tf_op jit(solution)/shard_map/all_gather | solution.py:85
  110.5 30.3 %cosine_bitcast_fusion = (f32[256,8,1024]{2,1,0:T(8,128)S(1)}, f32[256,8,1024]{2,1,0:T(8,128)S(1)}) fusion(f32[1024,256,8]{0,2,1:T(8,128)} %copy.72), kind=kLoop, calls=%fused_computation.5 | loop fusion | bytes 25165824 | tf_op jit(solution)/shard_map/dot_general | solution.py:64
  140.8 9.3 %fusion.2 = f32[64,256,8]{1,0,2:T(8,128)S(1)} fusion(f32[256,8,1024]{2,1,0:T(8,128)S(1)} %get-tuple-element.5, s32[64]{0:T(128)S(1)} %bitcast_add_fusion), kind=kOutput, calls=%fused_computation.2 | convolution fusion | flops 1610678272 | bytes 8913152 | tf_op jit(solution)/shard_map/dot_general | solution.py:64
  150.1 9.7 %fusion = f32[64,256,8]{1,0,2:T(8,128)S(1)} fusion(f32[256,8,1024]{2,1,0:T(8,128)S(1)} %get-tuple-element.6, s32[64]{0:T(128)S(1)} %bitcast_add_fusion), kind=kOutput, calls=%fused_computation | convolution fusion | flops 1610678272 | bytes 8913152 | tf_op jit(solution)/shard_map/dot_general | solution.py:70
  159.9 2.0 multiply_subtract_fusion
  161.9 1.6 fusion.31
  163.5 1.6 fusion.29
  165.0 1.7 fusion.10
  166.8 1.6 fusion.9
  169.0 68.6 %all_to_all.30 = f32[128,256,8]{0,2,1:T(8,128)S(1)} all-to-all(f32[128,256,8]{0,2,1:T(8,128)S(1)} %copy.82), channel_id=1, replica_groups=mesh['tile'=16,'depth'=32] {'depth'}, dimensions={1} | all-to-all | bytes 2097152 | tf_op jit(solution)/shard_map/all_to_all | solution.py:13
  238.6 1.6 fusion.18
  240.2 1.6 fusion.27
  242.1 1.6 fusion.8
  243.7 2.4 fusion.7
  (23 shorter events, 4.1 us)
Async XLA Ops:
  6.5 1.0 copy-start
  6.5 22.8 %copy-start.2 = (s32[64]{0:T(128)S(1)}, s32[64]{0:T(128)}, u32[]{:S(2)}) copy-start(s32[64]{0:T(128)} %param.6) | copy-start | bytes 772
  6.5 22.8 %copy-start.3 = (s32[64,1]{0,1:T(1,128)S(1)}, s32[64,1]{0,1:T(1,128)}, u32[]{:S(2)}) copy-start(s32[64,1]{0,1:T(1,128)} %param.5) | copy-start | bytes 772
  6.5 95.1 %all-gather.2.cloned.1.call-start = ((), (), s32[]{:S(2)}) async-start(), calls=%async_computation.2 | async-start | bytes 8912896 | tf_op jit(solution)/shard_map/all_gather | solution.py:85
  12.3 72.6 %all-to-all-start = ((f32[128,8,256]{0,1,2:T(8,128)}), f32[128,8,256]{0,1,2:T(8,128)S(1)}, u32[]{:S(2)}, u32[]{:S(2)}) async-start(f32[128,8,256]{0,1,2:T(8,128)} %copy.66), calls=%async_computation | async-start | bytes 2097152 | tf_op jit(solution)/shard_map/all_to_all | solution.py:13
  140.8 19.1 %copy-start.1 = (f32[64,8,256]{2,1,0:T(8,128)S(1)}, f32[64,8,256]{2,1,0:T(8,128)}, u32[]{:S(2)}) copy-start(f32[64,8,256]{2,1,0:T(8,128)} %fusion.33) | copy-start | bytes 1572868
Sparse Core Ops, SparseCore 0:
  10.3 91.2 all-gather.1
where the time goes:
time: 257 us; the launch traced here: 253 us
  blocking collectives  68.6 us (27%)
  waiting for transfers between devices  65.8 us (26%)
  local copies, waits for them, and re-layouts  44.4 us (17%)
  matrix products  43.2 us (17%)
  starting transfers between devices  17 us (7%)
  between operations  13.8 us (5%)
    all_to_all x1, blocking collectives, sent_together(): lax.all_to_all(both, axis, split_axis=split_dim, concat_axis=concat_dim,...  68.6 us
    all_to_all x1, waiting for transfers between devices, sent_together(): lax.all_to_all(both, axis, split_axis=split_dim, concat_axis=concat_dim,...  55.5 us
    dot_general x1, local copies, waits for them, and re-layouts, select_gains(): jnp.dot(selector, jnp.cos(flattened), precision=HIGHEST_PRECISION, prefer...  30.3 us
    all_to_all x1, starting transfers between devices, sent_together(): lax.all_to_all(both, axis, split_axis=split_dim, concat_axis=concat_dim,...  17 us
    dot_general x8, matrix products, apply_rows(): jnp.einsum('jk,skc->sjc', matrix, values, precision=HIGHEST_PRECISION, pr...  13.9 us
    dot_general x6, matrix products, right_apply(): jnp.einsum('src,ck->srk', values, matrix, precision=HIGHEST_PRECISION, pr...  10.3 us
    dot_general x1, matrix products, select_gains(): jnp.dot(selector, jnp.sin(flattened), precision=HIGHEST_PRECISION, prefer...  9.72 us
    all_gather x1, waiting for transfers between devices, on_device(): gathered = lax.all_gather(phases, 'tile', axis=0, tiled=True)  9.54 us
  transfers between devices with their start and end apart: 2, of which 2 were waited for; matrix products, arithmetic and copies ran while one was open for 5% of the time, Pallas kernels for 0%

commit v1 on v0

--- a/solution.py
+++ b/solution.py
@@ -5,6 +5,24 @@
 from jax.sharding import PartitionSpec as P
 
 HIGHEST_PRECISION = lax.Precision.HIGHEST
+
+
+def ring_gather(array, axis, dim):
+    ways, here, lap = (lax.axis_size(axis), lax.axis_index(axis), array.shape[dim])
+    lengths = [n * ways if d == dim else n for d, n in enumerate(array.shape)]
+    full = lax.dynamic_update_slice_in_dim(
+        jnp.zeros(lengths, array.dtype), array, here * lap, axis=dim
+    )
+    going_up = going_down = array
+    for far in range(1, ways // 2 + 1):
+        going_up = lax.ppermute(going_up, axis, [(d, (d + 1) % ways) for d in range(ways)])
+        full = lax.dynamic_update_slice_in_dim(full, going_up, (here - far) % ways * lap, axis=dim)
+        if 2 * far < ways:
+            going_down = lax.ppermute(going_down, axis, [(d, (d - 1) % ways) for d in range(ways)])
+            full = lax.dynamic_update_slice_in_dim(
+                full, going_down, (here + far) % ways * lap, axis=dim
+            )
+    return full
 
 
 def sent_together(arrays, axis, split_dim, concat_dim, along):
@@ -82,7 +100,7 @@
     levels = phases.shape[0]
     owners = lax.axis_size("tile")
     owner_column = patch_owner[:, 0]
-    gathered = lax.all_gather(phases, "tile", axis=0, tiled=True)
+    gathered = ring_gather(phases, "tile", 0)
     depth_index = owner_column * levels + patch_level
     depth_hot = (
         depth_index[:, None] == jnp.arange(owners * levels, dtype=jnp.int32)[None, :]

time: 257 us -> 755 us (2.94)
  the two profiles are of different devices: /device:TPU:1 before, /device:TPU:31 now
where the time goes in v1:
time: 755 us; the launch traced here: 747 us
  local copies, waits for them, and re-layouts  468 us (62%)
  starting transfers between devices  117 us (15%)
  blocking collectives  72.5 us (10%)
  matrix products  44.9 us (6%)
  waiting for transfers between devices  43.9 us (6%)
    dynamic_update_slice x8, local copies, waits for them, and re-layouts, ring_gather(): lax.dynamic_update_slice_in_dim(full, going_up, (here - far) % ways * lap...  204 us
    dynamic_update_slice x7, local copies, waits for them, and re-layouts, ring_gather(): lax.dynamic_update_slice_in_dim(full, going_down, (here + far) % ways * l...  163 us
    ppermute x8, starting transfers between devices, ring_gather(): lax.ppermute(going_up, axis, [(d, (d + 1) % ways) for d in range(ways)])  85.9 us
    all_to_all x1, blocking collectives, sent_together(): lax.all_to_all(both, axis, split_axis=split_dim, concat_axis=concat_dim,...  72.5 us
    ppermute x8, waiting for transfers between devices, ring_gather(): lax.ppermute(going_up, axis, [(d, (d + 1) % ways) for d in range(ways)])  43.9 us
    dynamic_update_slice x1, local copies, waits for them, and re-layouts, ring_gather(): lax.dynamic_update_slice_in_dim(jnp.zeros(lengths, array.dtype), array, h...  42.7 us
    dot_general x1, local copies, waits for them, and re-layouts, select_gains(): jnp.dot(selector, jnp.cos(flattened), precision=HIGHEST_PRECISION, prefer...  30.5 us
    all_to_all x1, starting transfers between devices, sent_together(): lax.all_to_all(both, axis, split_axis=split_dim, concat_axis=concat_dim,...  15.9 us
  transfers between devices with their start and end apart: 16, of which 6 were waited for; matrix products, arithmetic and copies ran while one was open for 53% of the time, Pallas kernels for 0%

profile of v1, /device:TPU:31, one launch (start us, length us, event | category | flops | bytes accessed | tf_op | source)
XLA Modules:
  0.0 747.3 jit_solution(8789301310299569675)
XLA Ops:
  5.7 15.9 %all-to-all-start = ((f32[128,8,256]{0,1,2:T(8,128)}), f32[128,8,256]{0,1,2:T(8,128)S(1)}, u32[]{:S(2)}, u32[]{:S(2)}) async-start(f32[128,8,256]{0,1,2:T(8,128)} %copy.82), calls=%async_computation | async-start | bytes 2097152 | tf_op jit(solution)/shard_map/all_to_all | solution.py:31
  27.0 9.9 %collective-permute-done = f32[64,256,8]{1,2,0:T(8,128)} collective-permute-done((f32[64,256,8]{1,2,0:T(8,128)S(1)}, f32[64,256,8]{1,2,0:T(8,128)}, u32[]{:S(2)}, u32[]{:S(2)}) %collective-permute-start) | collective-permute-done | bytes 524320 | tf_op jit(solution)/shard_map/ppermute | solution.py:18
  44.3 8.7 %collective-permute-done.2 = f32[64,256,8]{1,2,0:T(8,128)} collective-permute-done((f32[64,256,8]{1,2,0:T(8,128)}, f32[64,256,8]{1,2,0:T(8,128)}, u32[]{:S(2)}, u32[]{:S(2)}) %collective-permute-start.2) | collective-permute-done | bytes 524320 | tf_op jit(solution)/shard_map/ppermute | solution.py:18
  62.3 7.8 %collective-permute-done.4 = f32[64,256,8]{1,2,0:T(8,128)S(1)} collective-permute-done((f32[64,256,8]{1,2,0:T(8,128)}, f32[64,256,8]{1,2,0:T(8,128)S(1)}, u32[]{:S(2)}, u32[]{:S(2)}) %collective-permute-start.4) | collective-permute-done | bytes 524320 | tf_op jit(solution)/shard_map/ppermute | solution.py:18
  130.3 42.7 %dynamic_update_slice.48 = f32[1024,256,8]{0,2,1:T(8,128)} dynamic-update-slice(f32[1024,256,8]{0,2,1:T(8,128)} %broadcast_in_dim.2, f32[64,256,8]{0,2,1:T(8,128)S(1)} %copy.88, s32[]{:T(128)S(6)} %select_n.144, s32[]{:T(128)} %constant.105.clone.1, s32[]{:T(128)} %constant.105.clone.1) | dynamic-update-slice | bytes 1048580 | tf_op jit(solution)/shard_map/dynamic_update_slice | solution.py:13
  182.6 8.4 %dynamic_update_slice.50 = f32[1024,256,8]{0,2,1:T(8,128)} dynamic-update-slice(f32[1024,256,8]{0,2,1:T(8,128)} %dynamic_update_slice.49, f32[64,256,8]{0,2,1:T(8,128)S(1)} %copy.90, s32[]{:T(128)S(6)} %select_n.148, s32[]{:T(128)} %constant.105.clone.1, s32[]{:T(128)} %constant.105.clone.1) | dynamic-update-slice | bytes 1048580 | tf_op jit(solution)/shard_map/dynamic_update_slice | solution.py:22
  192.5 42.9 %dynamic_update_slice.51 = f32[1024,256,8]{0,2,1:T(8,128)} dynamic-update-slice(f32[1024,256,8]{0,2,1:T(8,128)} %dynamic_update_slice.50, f32[64,256,8]{0,2,1:T(8,128)S(1)} %copy.91, s32[]{:T(128)S(6)} %select_n.150, s32[]{:T(128)} %constant.105.clone.1, s32[]{:T(128)} %constant.105.clone.1) | dynamic-update-slice | bytes 1048580 | tf_op jit(solution)/shard_map/dynamic_update_slice | solution.py:19
  236.9 42.9 %dynamic_update_slice.52 = f32[1024,256,8]{0,2,1:T(8,128)} dynamic-update-slice(f32[1024,256,8]{0,2,1:T(8,128)} %dynamic_update_slice.51, f32[64,256,8]{0,2,1:T(8,128)S(1)} %copy.92, s32[]{:T(128)S(6)} %select_n.152, s32[]{:T(128)} %constant.105.clone.1, s32[]{:T(128)} %constant.105.clone.1) | dynamic-update-slice | bytes 1048580 | tf_op jit(solution)/shard_map/dynamic_update_slice | solution.py:22
  280.3 8.4 %dynamic_update_slice.53 = f32[1024,256,8]{0,2,1:T(8,128)} dynamic-update-slice(f32[1024,256,8]{0,2,1:T(8,128)} %dynamic_update_slice.52, f32[64,256,8]{0,2,1:T(8,128)S(1)} %copy.93, s32[]{:T(128)S(6)} %select_n.154, s32[]{:T(128)} %constant.105.clone.1, s32[]{:T(128)} %constant.105.clone.1) | dynamic-update-slice | bytes 1048580 | tf_op jit(solution)/shard_map/dynamic_update_slice | solution.py:19
  290.2 8.4 %dynamic_update_slice.54 = f32[1024,256,8]{0,2,1:T(8,128)} dynamic-update-slice(f32[1024,256,8]{0,2,1:T(8,128)} %dynamic_update_slice.53, f32[64,256,8]{0,2,1:T(8,128)S(1)} %copy.94, s32[]{:T(128)S(6)} %select_n.156, s32[]{:T(128)} %constant.105.clone.1, s32[]{:T(128)} %constant.105.clone.1) | dynamic-update-slice | bytes 1048580 | tf_op jit(solution)/shard_map/dynamic_update_slice | solution.py:22
  300.0 42.9 %dynamic_update_slice.55 = f32[1024,256,8]{0,2,1:T(8,128)} dynamic-update-slice(f32[1024,256,8]{0,2,1:T(8,128)} %dynamic_update_slice.54, f32[64,256,8]{0,2,1:T(8,128)S(1)} %copy.95, s32[]{:T(128)S(6)} %select_n.158, s32[]{:T(128)} %constant.105.clone.1, s32[]{:T(128)} %constant.105.clone.1) | dynamic-update-slice | bytes 1048580 | tf_op jit(solution)/shard_map/dynamic_update_slice | solution.py:19
  343.4 43.1 %dynamic_update_slice.56 = f32[1024,256,8]{0,2,1:T(8,128)} dynamic-update-slice(f32[1024,256,8]{0,2,1:T(8,128)} %dynamic_update_slice.55, f32[64,256,8]{0,2,1:T(8,128)S(1)} %copy.96, s32[]{:T(128)S(6)} %select_n.160, s32[]{:T(128)} %constant.105.clone.1, s32[]{:T(128)} %constant.105.clone.1) | dynamic-update-slice | bytes 1048580 | tf_op jit(solution)/shard_map/dynamic_update_slice | solution.py:22
  388.0 8.3 %dynamic_update_slice.57 = f32[1024,256,8]{0,2,1:T(8,128)} dynamic-update-slice(f32[1024,256,8]{0,2,1:T(8,128)} %dynamic_update_slice.56, f32[64,256,8]{0,2,1:T(8,128)S(1)} %copy.97, s32[]{:T(128)S(6)} %select_n.162, s32[]{:T(128)} %constant.105.clone.1, s32[]{:T(128)} %constant.105.clone.1) | dynamic-update-slice | bytes 1048580 | tf_op jit(solution)/shard_map/dynamic_update_slice | solution.py:19
  397.8 8.4 %dynamic_update_slice.58 = f32[1024,256,8]{0,2,1:T(8,128)} dynamic-update-slice(f32[1024,256,8]{0,2,1:T(8,128)} %dynamic_update_slice.57, f32[64,256,8]{0,2,1:T(8,128)S(1)} %copy.98, s32[]{:T(128)S(6)} %select_n.164, s32[]{:T(128)} %constant.105.clone.1, s32[]{:T(128)} %constant.105.clone.1) | dynamic-update-slice | bytes 1048580 | tf_op jit(solution)/shard_map/dynamic_update_slice | solution.py:22
  407.6 42.9 %dynamic_update_slice.59 = f32[1024,256,8]{0,2,1:T(8,128)} dynamic-update-slice(f32[1024,256,8]{0,2,1:T(8,128)} %dynamic_update_slice.58, f32[64,256,8]{0,2,1:T(8,128)S(1)} %copy.99, s32[]{:T(128)S(6)} %select_n.166, s32[]{:T(128)} %constant.105.clone.1, s32[]{:T(128)} %constant.105.clone.1) | dynamic-update-slice | bytes 1048580 | tf_op jit(solution)/shard_map/dynamic_update_slice | solution.py:19
  451.0 43.0 %dynamic_update_slice.60 = f32[1024,256,8]{0,2,1:T(8,128)} dynamic-update-slice(f32[1024,256,8]{0,2,1:T(8,128)} %dynamic_update_slice.59, f32[64,256,8]{0,2,1:T(8,128)S(1)} %copy.100, s32[]{:T(128)S(6)} %select_n.168, s32[]{:T(128)} %constant.105.clone.1, s32[]{:T(128)} %constant.105.clone.1) | dynamic-update-slice | bytes 1048580 | tf_op jit(solution)/shard_map/dynamic_update_slice | solution.py:22
  495.4 8.3 %dynamic_update_slice.61 = f32[1024,256,8]{0,2,1:T(8,128)} dynamic-update-slice(f32[1024,256,8]{0,2,1:T(8,128)} %dynamic_update_slice.60, f32[64,256,8]{0,2,1:T(8,128)S(1)} %copy.101, s32[]{:T(128)S(6)} %select_n.170, s32[]{:T(128)} %constant.105.clone.1, s32[]{:T(128)} %constant.105.clone.1) | dynamic-update-slice | bytes 1048580 | tf_op jit(solution)/shard_map/dynamic_update_slice | solution.py:19
  505.3 8.4 %dynamic_update_slice.62 = f32[1024,256,8]{0,2,1:T(8,128)} dynamic-update-slice(f32[1024,256,8]{0,2,1:T(8,128)} %dynamic_update_slice.61, f32[64,256,8]{0,2,1:T(8,128)S(1)} %copy.102, s32[]{:T(128)S(6)} %select_n.172, s32[]{:T(128)} %constant.105.clone.1, s32[]{:T(128)} %constant.105.clone.1) | dynamic-update-slice | bytes 1048580 | tf_op jit(solution)/shard_map/dynamic_update_slice | solution.py:22
  513.6 41.5 %collective-permute-start.14 = (f32[64,256,8]{1,2,0:T(8,128)}, f32[64,256,8]{1,2,0:T(8,128)S(1)}, u32[]{:S(2)}, u32[]{:S(2)}) collective-permute-start(f32[64,256,8]{1,2,0:T(8,128)} %collective-permute-done.12), channel_id=1, source_target_pairs={{0,32},{32,64},{64,96},{96,128},{128,160},{160,192},{192,224},{224... | collective-permute-start | bytes 1572872 | tf_op jit(solution)/shard_map/ppermute | solution.py:18
  564.7 42.9 %dynamic_update_slice.63 = f32[1024,256,8]{0,2,1:T(8,128)} dynamic-update-slice(f32[1024,256,8]{0,2,1:T(8,128)} %dynamic_update_slice.62, f32[64,256,8]{0,2,1:T(8,128)S(1)} %copy.103, s32[]{:T(128)S(6)} %select_n.174, s32[]{:T(128)} %constant.105.clone.1, s32[]{:T(128)} %constant.105.clone.1) | dynamic-update-slice | bytes 1048580 | tf_op jit(solution)/shard_map/dynamic_update_slice | solution.py:19
  607.6 30.5 %cosine_bitcast_fusion = (f32[256,8,1024]{2,1,0:T(8,128)S(1)}, f32[256,8,1024]{2,1,0:T(8,128)S(1)}) fusion(f32[1024,256,8]{0,2,1:T(8,128)} %dynamic_update_slice.63), kind=kLoop, calls=%fused_computation.5 | loop fusion | bytes 25165824 | tf_op jit(solution)/shard_map/dot_general | solution.py:82
  638.1 9.3 %fusion = f32[64,256,8]{1,0,2:T(8,128)S(1)} fusion(f32[256,8,1024]{2,1,0:T(8,128)S(1)} %get-tuple-element.6, s32[64]{0:T(128)S(1)} %bitcast_add_fusion), kind=kOutput, calls=%fused_computation | convolution fusion | flops 1610678272 | bytes 8913152 | tf_op jit(solution)/shard_map/dot_general | solution.py:88
  647.5 9.5 %fusion.2 = f32[64,256,8]{1,0,2:T(8,128)S(1)} fusion(f32[256,8,1024]{2,1,0:T(8,128)S(1)} %get-tuple-element.5, s32[64]{0:T(128)S(1)} %bitcast_add_fusion), kind=kOutput, calls=%fused_computation.2 | convolution fusion | flops 1610678272 | bytes 8913152 | tf_op jit(solution)/shard_map/dot_general | solution.py:82
  666.1 72.5 %all_to_all.30 = f32[128,256,8]{0,2,1:T(8,128)S(1)} all-to-all(f32[128,256,8]{0,2,1:T(8,128)S(1)} %copy.112), channel_id=1, replica_groups=mesh['tile'=16,'depth'=32] {'depth'}, dimensions={1} | all-to-all | bytes 2097152 | tf_op jit(solution)/shard_map/all_to_all | solution.py:31
  (106 shorter events, 138.4 us)
Async XLA Ops:
  4.4 168.6 %copy-start.14 = (s32[64]{0:T(128)S(1)}, s32[64]{0:T(128)}, u32[]{:S(2)}) copy-start(s32[64]{0:T(128)} %param.6) | copy-start | bytes 772
  4.4 168.6 %copy-start.15 = (s32[64,1]{0,1:T(1,128)S(1)}, s32[64,1]{0,1:T(1,128)}, u32[]{:S(2)}) copy-start(s32[64,1]{0,1:T(1,128)} %param.5) | copy-start | bytes 772
  5.7 549.3 %all-to-all-start = ((f32[128,8,256]{0,1,2:T(8,128)}), f32[128,8,256]{0,1,2:T(8,128)S(1)}, u32[]{:S(2)}, u32[]{:S(2)}) async-start(f32[128,8,256]{0,1,2:T(8,128)} %copy.82), calls=%async_computation | async-start | bytes 2097152 | tf_op jit(solution)/shard_map/all_to_all | solution.py:31
  21.7 15.2 %collective-permute-start = (f32[64,256,8]{1,2,0:T(8,128)S(1)}, f32[64,256,8]{1,2,0:T(8,128)}, u32[]{:S(2)}, u32[]{:S(2)}) collective-permute-start(f32[64,256,8]{1,2,0:T(8,128)S(1)} %copy-done.2), channel_id=1, source_target_pairs={{0,32},{32,64},{64,96},{96,128},{128,160},{160,192},{192,224},{224... | collective-permute-start | bytes 1572872 | tf_op jit(solution)/shard_map/ppermute | solution.py:18
  23.6 18.7 %collective-permute-start.1 = (f32[64,256,8]{1,2,0:T(8,128)S(1)}, f32[64,256,8]{1,2,0:T(8,128)S(1)}, u32[]{:S(2)}, u32[]{:S(2)}) collective-permute-start(f32[64,256,8]{1,2,0:T(8,128)S(1)} %copy-done.2), channel_id=1, source_target_pairs={{0,480},{32,0},{64,32},{96,64},{128,96},{160,128},{192,160},{224,1... | collective-permute-start | bytes 1572872 | tf_op jit(solution)/shard_map/ppermute | solution.py:21
  36.9 16.0 %collective-permute-start.2 = (f32[64,256,8]{1,2,0:T(8,128)}, f32[64,256,8]{1,2,0:T(8,128)}, u32[]{:S(2)}, u32[]{:S(2)}) collective-permute-start(f32[64,256,8]{1,2,0:T(8,128)} %collective-permute-done), channel_id=1, source_target_pairs={{0,32},{32,64},{64,96},{96,128},{128,160},{160,192},{192,224},{224... | collective-permute-start | bytes 1572872 | tf_op jit(solution)/shard_map/ppermute | solution.py:18
  42.3 66.4 %copy-start.3 = (f32[64,256,8]{1,2,0:T(8,128)}, f32[64,256,8]{1,2,0:T(8,128)S(1)}, u32[]{:S(2)}) copy-start(f32[64,256,8]{1,2,0:T(8,128)S(1)} %collective-permute-done.1) | copy-start | bytes 1572868
  42.3 18.0 %collective-permute-start.3 = (f32[64,256,8]{1,2,0:T(8,128)S(1)}, f32[64,256,8]{1,2,0:T(8,128)}, u32[]{:S(2)}, u32[]{:S(2)}) collective-permute-start(f32[64,256,8]{1,2,0:T(8,128)S(1)} %collective-permute-done.1), channel_id=1, source_target_pairs={{0,480},{32,0},{64,32},{96,64},{128,96},{160,128},{192,160},{224,1... | collective-permute-start | bytes 1572872 | tf_op jit(solution)/shard_map/ppermute | solution.py:21
  53.0 17.2 %collective-permute-start.4 = (f32[64,256,8]{1,2,0:T(8,128)}, f32[64,256,8]{1,2,0:T(8,128)S(1)}, u32[]{:S(2)}, u32[]{:S(2)}) collective-permute-start(f32[64,256,8]{1,2,0:T(8,128)} %collective-permute-done.2), channel_id=1, source_target_pairs={{0,32},{32,64},{64,96},{96,128},{128,160},{160,192},{192,224},{224... | collective-permute-start | bytes 1572872 | tf_op jit(solution)/shard_map/ppermute | solution.py:18
  60.4 17.1 %collective-permute-start.5 = (f32[64,256,8]{1,2,0:T(8,128)}, f32[64,256,8]{1,2,0:T(8,128)S(1)}, u32[]{:S(2)}, u32[]{:S(2)}) collective-permute-start(f32[64,256,8]{1,2,0:T(8,128)} %collective-permute-done.3), channel_id=1, source_target_pairs={{0,480},{32,0},{64,32},{96,64},{128,96},{160,128},{192,160},{224,1... | collective-permute-start | bytes 1572872 | tf_op jit(solution)/shard_map/ppermute | solution.py:21
  70.2 55.0 %copy-start.5 = (f32[64,256,8]{1,2,0:T(8,128)}, f32[64,256,8]{1,2,0:T(8,128)S(1)}, u32[]{:S(2)}) copy-start(f32[64,256,8]{1,2,0:T(8,128)S(1)} %collective-permute-done.4) | copy-start | bytes 1572868
  70.2 15.9 %collective-permute-start.6 = (f32[64,256,8]{1,2,0:T(8,128)S(1)}, f32[64,256,8]{1,2,0:T(8,128)S(1)}, u32[]{:S(2)}, u32[]{:S(2)}) collective-permute-start(f32[64,256,8]{1,2,0:T(8,128)S(1)} %collective-permute-done.4), channel_id=1, source_target_pairs={{0,32},{32,64},{64,96},{96,128},{128,160},{160,192},{192,224},{224... | collective-permute-start | bytes 1572872 | tf_op jit(solution)/shard_map/ppermute | solution.py:18
  77.5 47.7 %copy-start.7 = (f32[64,256,8]{1,2,0:T(8,128)}, f32[64,256,8]{1,2,0:T(8,128)S(1)}, u32[]{:S(2)}) copy-start(f32[64,256,8]{1,2,0:T(8,128)S(1)} %collective-permute-done.5) | copy-start | bytes 1572868
  77.5 16.0 %collective-permute-start.7 = (f32[64,256,8]{1,2,0:T(8,128)S(1)}, f32[64,256,8]{1,2,0:T(8,128)S(1)}, u32[]{:S(2)}, u32[]{:S(2)}) collective-permute-start(f32[64,256,8]{1,2,0:T(8,128)S(1)} %collective-permute-done.5), channel_id=1, source_target_pairs={{0,480},{32,0},{64,32},{96,64},{128,96},{160,128},{192,160},{224,1... | collective-permute-start | bytes 1572872 | tf_op jit(solution)/shard_map/ppermute | solution.py:21
  86.1 15.2 %collective-permute-start.8 = (f32[64,256,8]{1,2,0:T(8,128)S(1)}, f32[64,256,8]{1,2,0:T(8,128)S(1)}, u32[]{:S(2)}, u32[]{:S(2)}) collective-permute-start(f32[64,256,8]{1,2,0:T(8,128)S(1)} %collective-permute-done.6), channel_id=1, source_target_pairs={{0,32},{32,64},{64,96},{96,128},{128,160},{160,192},{192,224},{224... | collective-permute-start | bytes 1572872 | tf_op jit(solution)/shard_map/ppermute | solution.py:18
  93.5 15.2 %collective-permute-start.9 = (f32[64,256,8]{1,2,0:T(8,128)S(1)}, f32[64,256,8]{1,2,0:T(8,128)S(1)}, u32[]{:S(2)}, u32[]{:S(2)}) collective-permute-start(f32[64,256,8]{1,2,0:T(8,128)S(1)} %collective-permute-done.7), channel_id=1, source_target_pairs={{0,480},{32,0},{64,32},{96,64},{128,96},{160,128},{192,160},{224,1... | collective-permute-start | bytes 1572872 | tf_op jit(solution)/shard_map/ppermute | solution.py:21
  101.3 14.3 %collective-permute-start.10 = (f32[64,256,8]{1,2,0:T(8,128)S(1)}, f32[64,256,8]{1,2,0:T(8,128)}, u32[]{:S(2)}, u32[]{:S(2)}) collective-permute-start(f32[64,256,8]{1,2,0:T(8,128)S(1)} %collective-permute-done.8), channel_id=1, source_target_pairs={{0,32},{32,64},{64,96},{96,128},{128,160},{160,192},{192,224},{224... | collective-permute-start | bytes 1572872 | tf_op jit(solution)/shard_map/ppermute | solution.py:18
  108.7 14.4 %collective-permute-start.11 = (f32[64,256,8]{1,2,0:T(8,128)S(1)}, f32[64,256,8]{1,2,0:T(8,128)S(1)}, u32[]{:S(2)}, u32[]{:S(2)}) collective-permute-start(f32[64,256,8]{1,2,0:T(8,128)S(1)} %collective-permute-done.9), channel_id=1, source_target_pairs={{0,480},{32,0},{64,32},{96,64},{128,96},{160,128},{192,160},{224,1... | collective-permute-start | bytes 1572872 | tf_op jit(solution)/shard_map/ppermute | solution.py:21
  115.6 378.4 %collective-permute-start.12 = (f32[64,256,8]{1,2,0:T(8,128)}, f32[64,256,8]{1,2,0:T(8,128)}, u32[]{:S(2)}, u32[]{:S(2)}) collective-permute-start(f32[64,256,8]{1,2,0:T(8,128)} %collective-permute-done.10), channel_id=1, source_target_pairs={{0,32},{32,64},{64,96},{96,128},{128,160},{160,192},{192,224},{224... | collective-permute-start | bytes 1572872 | tf_op jit(solution)/shard_map/ppermute | solution.py:18
  123.2 380.6 %collective-permute-start.13 = (f32[64,256,8]{1,2,0:T(8,128)S(1)}, f32[64,256,8]{1,2,0:T(8,128)}, u32[]{:S(2)}, u32[]{:S(2)}) collective-permute-start(f32[64,256,8]{1,2,0:T(8,128)S(1)} %collective-permute-done.11), channel_id=1, source_target_pairs={{0,480},{32,0},{64,32},{96,64},{128,96},{160,128},{192,160},{224,1... | collective-permute-start | bytes 1572872 | tf_op jit(solution)/shard_map/ppermute | solution.py:21
  125.6 56.5 %copy-start.4 = (f32[64,256,8]{1,2,0:T(8,128)S(1)}, f32[64,256,8]{1,2,0:T(8,128)}, u32[]{:S(2)}) copy-start(f32[64,256,8]{1,2,0:T(8,128)} %copy-done.3) | copy-start | bytes 1572868
  182.6 97.2 %copy-start.6 = (f32[64,256,8]{1,2,0:T(8,128)S(1)}, f32[64,256,8]{1,2,0:T(8,128)}, u32[]{:S(2)}) copy-start(f32[64,256,8]{1,2,0:T(8,128)} %copy-done.5) | copy-start | bytes 1572868
  280.3 62.6 %copy-start.10 = (f32[64,256,8]{1,2,0:T(8,128)S(1)}, f32[64,256,8]{1,2,0:T(8,128)}, u32[]{:S(2)}) copy-start(f32[64,256,8]{1,2,0:T(8,128)} %copy-done.9) | copy-start | bytes 1572868
  513.6 50.6 %collective-permute-start.14 = (f32[64,256,8]{1,2,0:T(8,128)}, f32[64,256,8]{1,2,0:T(8,128)S(1)}, u32[]{:S(2)}, u32[]{:S(2)}) collective-permute-start(f32[64,256,8]{1,2,0:T(8,128)} %collective-permute-done.12), channel_id=1, source_target_pairs={{0,32},{32,64},{64,96},{96,128},{128,160},{160,192},{192,224},{224... | collective-permute-start | bytes 1572872 | tf_op jit(solution)/shard_map/ppermute | solution.py:18
  (8 other events, 158.8 us)
